TPU v7x, 256 devices: a whole 4x4x8 slice. The times are simulated.
256 devices in a mesh: fft: 16 (over z, x_lo), pair: 16 (over y, x_hi, core).
Axes of the slice: x: 4 (x_hi: 2, x_lo: 2; x = x_hi * 2 + x_lo), y: 4, z: 8, core: 2. Of those that a mesh axis runs over, the one named last changes fastest.
Arguments:
- virt_orbitals: bfloat16 [1024, 96, 9216], P('pair', 'fft'), may hold values from -6 to 6
- occ_orbitals: bfloat16 [8, 96, 9216], P(None, 'fft'), may hold values from -6 to 6
- occ_index: int32 [1], replicated, may hold values from 0 to 7
- occ_energy: float32 [8], replicated, may hold values from -1.2 to -0.3
- band_energy: float32 [1024], replicated, may hold values from 0.1 to 3
- geminal_exponent: float32 [1], replicated, may hold values from 1.5 to 4
- pencil_index: int32 [1536], replicated, may hold values from 0 to 4703, as said below
- block_owner: int32 [16], replicated, may hold values from 0 to 15, each once
Outputs:
- pair_matrix: float32 [1024, 1024], P('pair', 'fft')
Inputs may be any that keep to these rules, and one draw needn't show every extreme that they name: `pencil_index`: distinct and ascending; entry n names the pencil of second frequency pencil_index[n] // 49 and third frequency pencil_index[n] % 49 - 24. `block_owner`: a permutation of the band blocks.
All inputs are finite; a program needn't handle non-finite values.
Results may differ from a plain program's by a relative error of at most 0.0015.
The roundings to bfloat16 on the way count: a program that leaves them out, or rounds other values in their place, can miss the bound.
Values may be sent and summed in bfloat16 or wider, within the bound.
No kernel may reach another device: no remote copies, remote signals or barrier semaphores. Data moves between devices by JAX's collectives and lax.ppermute only.
A program may use at most 128 MiB of HBM per device.

v0:
```python
import math

import jax
import jax.numpy as jnp
from jax import lax
from jax.sharding import PartitionSpec as P

G = 96
R = 24
KZ = 49
NPEN = 1536
NBAND = 1024
OCC = 1


def cut_along(shard, dim, size):
    shape = shard.shape
    blocks = shard.reshape(*shape[:dim], size, shape[dim] // size, *shape[dim + 1 :])
    return jnp.moveaxis(blocks, dim, 0)


def in_order(blocks, dim):
    shape = list(blocks.shape[1:])
    shape[dim] *= blocks.shape[0]
    return jnp.moveaxis(blocks, 0, dim).reshape(shape)


def one_exchange(shard, axis, axes, splits, concats):
    sizes = [lax.axis_size(a) for a in axes]
    blocks = cut_along(shard, splits[0], sizes[0])
    blocks = jnp.moveaxis(cut_along(blocks, splits[1] + 1, sizes[1]), 0, 1)
    inside = blocks.shape[2:]
    blocks = blocks.reshape(-1, *inside)
    blocks = lax.all_to_all(blocks, axis, split_axis=0, concat_axis=0, tiled=True)
    blocks = in_order(blocks.reshape(*sizes, *inside), concats[0] + 1)
    return in_order(blocks, concats[1])


def sent_and_summed(shard, axis, dim):
    blocks = cut_along(shard, dim, lax.axis_size(axis))
    arrived = lax.all_to_all(blocks, axis, split_axis=0, concat_axis=0, tiled=True)
    return arrived.sum(axis=0)


def phase_tables(length, offset, columns):
    grid_rows = jnp.arange(length, dtype=jnp.int32)[:, None]
    grid_cols = jnp.arange(columns, dtype=jnp.int32)[None, :] - offset
    turns = jnp.mod(grid_rows * grid_cols, length).astype(jnp.float32)
    angle = turns * (2.0 * math.pi / length)
    return (jnp.cos(angle), jnp.sin(angle))


def forward_tables():
    cos_z, sin_z = phase_tables(G, R, KZ)
    z_table = jnp.concatenate([cos_z, -sin_z], axis=1).astype(jnp.bfloat16)
    cos_g, sin_g = phase_tables(G, 0, G)
    cos_b = cos_g.astype(jnp.bfloat16)
    sin_b = sin_g.astype(jnp.bfloat16)
    to_real = jnp.stack([cos_b, sin_b], axis=1)
    to_imag = jnp.stack([-sin_b, cos_b], axis=1)
    plane_table = jnp.stack([to_real, to_imag], axis=3)
    return (z_table, cos_b, sin_b, plane_table)


def half_kernel(exponent, kept_pens):
    freq_x = jnp.mod(jnp.arange(G, dtype=jnp.int32) + G // 2, G) - G // 2
    freq_y = jnp.mod(kept_pens // KZ + G // 2, G) - G // 2
    freq_z = kept_pens % KZ - R
    squared = (freq_x * freq_x)[:, None] + (freq_y * freq_y + freq_z * freq_z)[None, :]
    squared = squared.astype(jnp.float32)
    return 1.0 / ((G * exponent) ** 1.5 * (1.0 + squared / (exponent * exponent)))


def plane_coefficients(virtual, occupied, z_table, plane_table, pencils):
    bands, planes = (virtual.shape[0], virtual.shape[1])
    density = (occupied.astype(jnp.float32)[None] * virtual.astype(jnp.float32)).astype(
        jnp.bfloat16
    )
    z_coeffs = jnp.dot(
        density.reshape(bands * planes * G, G), z_table, preferred_element_type=jnp.float32
    )
    z_coeffs = z_coeffs.astype(jnp.bfloat16).reshape(bands * planes, G, 2, KZ)
    transformed = jnp.einsum(
        "mycj,ycko->mokj", z_coeffs, plane_table, preferred_element_type=jnp.float32
    ).astype(jnp.bfloat16)
    chosen = transformed[:, :, pencils // KZ, pencils % KZ]
    real_part = chosen[:, 0].reshape(bands, planes, pencils.shape[0])
    imag_part = chosen[:, 1].reshape(bands, planes, pencils.shape[0])
    return (real_part, imag_part)


def spectral(real_part, imag_part, cos_g, sin_g, weight):
    columns = real_part.shape[-1]
    stacked = jnp.concatenate([real_part, imag_part], axis=-1)
    cos_terms = jnp.einsum("...xn,xk->...kn", stacked, cos_g, preferred_element_type=jnp.float32)
    sin_terms = jnp.einsum("...xn,xk->...kn", stacked, sin_g, preferred_element_type=jnp.float32)
    weighted_re = ((cos_terms[..., :columns] + sin_terms[..., columns:]) * weight).astype(
        jnp.bfloat16
    )
    weighted_im = ((cos_terms[..., columns:] - sin_terms[..., :columns]) * weight).astype(
        jnp.bfloat16
    )
    return (weighted_re, weighted_im)


def body(
    virt_orbitals,
    occ_orbitals,
    occ_index,
    occ_energy,
    band_energy,
    geminal_exponent,
    pencil_index,
    block_owner,
):
    fft_count = lax.axis_size("fft")
    pair_count = lax.axis_size("pair")
    bands_here = NBAND // pair_count
    z_table, cos_g, sin_g, plane_table = forward_tables()
    number = 0
    occupied = lax.dynamic_index_in_dim(occ_orbitals, occ_index[number], 0, keepdims=False)
    real_part, imag_part = plane_coefficients(
        virt_orbitals, occupied, z_table, plane_table, pencil_index
    )
    real_parts = [real_part]
    imag_parts = [imag_part]
    chosen_re = jnp.stack(real_parts)
    chosen_im = jnp.stack(imag_parts)
    exponent = geminal_exponent[0]
    whole_re, whole_im = (
        one_exchange(chosen_re, ("fft", "pair"), ("fft", "pair"), (3, 3), (2, 1)),
        one_exchange(chosen_im, ("fft", "pair"), ("fft", "pair"), (3, 3), (2, 1)),
    )
    pen_count = NPEN // (fft_count * pair_count)
    pen_start = (lax.axis_index("fft") * pair_count + lax.axis_index("pair")) * pen_count
    kept_pens = lax.dynamic_slice_in_dim(pencil_index, pen_start, pen_count)
    coeff_re, coeff_im = spectral(
        whole_re, whole_im, cos_g, sin_g, half_kernel(exponent, kept_pens)
    )
    flat_re = coeff_re.reshape(OCC, NBAND, -1)
    flat_im = coeff_im.reshape(OCC, NBAND, -1)
    joined = jnp.concatenate([flat_re, flat_im], axis=2)
    terms = joined.shape[2]
    owned = jnp.take(
        joined.reshape(OCC, pair_count, bands_here, terms), block_owner, axis=1
    ).reshape(OCC, NBAND, terms)
    energy_owned = jnp.take(
        band_energy.reshape(pair_count, bands_here), block_owner, axis=0
    ).reshape(NBAND)
    occ_chosen = jnp.take(occ_energy, occ_index)
    number = 0
    gram = jnp.einsum(
        "rk,ck->rc", owned[number], joined[number], preferred_element_type=jnp.float32
    )
    factor = energy_owned[:, None] + band_energy[None, :] - 2.0 * occ_chosen[number]
    combined = factor * gram
    row_sums = sent_and_summed(combined, "pair", 0)
    return sent_and_summed(row_sums, "fft", 1)


def solution(mesh):
    return jax.shard_map(
        body,
        mesh=mesh,
        in_specs=(P("pair", "fft", None), P(None, "fft", None), P(), P(), P(), P(), P(), P()),
        out_specs=P("pair", "fft"),
        check_vma=False,
    )
```

profile of v0, /device:TPU:2, one launch (start us, length us, event | category | flops | bytes accessed | tf_op | source)
XLA Modules:
  0.0 347.5 jit_solution(6593627230097250328)
XLA Ops:
  1.5 7.6 %multiply_convert_fusion = bf16[64,6,9216]{2,0,1:T(8,128)(2,1)} fusion(bf16[64,6,9216]{2,0,1:T(8,128)(2,1)} %param.8, f32[6,9216]{1,0:T(8,128)S(1)} %fusion.12), kind=kLoop, calls=%fused_computation.5 | loop fusion | flops 10616832 | bytes 14376960 | tf_op jit(solution)/shard_map/convert_element_type | solution.py:76
  9.1 10.6 %copy.81 = bf16[64,6,9216]{2,1,0:T(8,128)(2,1)} copy(bf16[64,6,9216]{2,0,1:T(8,128)(2,1)} %multiply_convert_fusion) | data formatting | bytes 14155776 | tf_op jit(solution)/shard_map/convert_element_type | solution.py:76
  19.7 16.7 %reshape.236 = bf16[36864,96]{1,0:T(8,128)(2,1)} reshape(bf16[64,6,9216]{2,1,0:T(8,128)(2,1)} %copy.81) | data formatting | bytes 14155776 | tf_op jit(solution)/shard_map/reshape | solution.py:80
  36.7 10.0 %convolution_convert_fusion = bf16[36864,98]{0,1:T(8,128)(2,1)} fusion(bf16[36864,96]{1,0:T(8,128)(2,1)} %reshape.236, bf16[96,49]{1,0:T(8,128)(2,1)S(1)} %get-tuple-element.23, bf16[96,49]{1,0:T(8,128)(2,1)S(1)} %get-tuple-element.22), kind=kOutput, calls=%fused_computation.3 | convolution fusion | flops 697283328 | bytes 14322048 | tf_op jit(solution)/shard_map/dot_general | solution.py:79
  46.7 15.0 %reshape.237 = bf16[384,96,2,49]{1,0,3,2:T(8,128)(2,1)} reshape(bf16[36864,98]{0,1:T(8,128)(2,1)} %convolution_convert_fusion) | data formatting | bytes 14450688 | tf_op jit(solution)/shard_map/reshape | solution.py:82
  61.7 9.9 %fusion.2 = bf16[384,2,96,49]{0,2,3,1:T(8,128)(2,1)} fusion(bf16[384,96,2,49]{1,0,3,2:T(8,128)(2,1)} %reshape.237, bf16[96,2,96,1]{0,2,1,3:T(8,128)(2,1)S(1)} %get-tuple-element.21, bf16[96,2,96,1]{0,2,1,3:T(8,128)(2,1)S(1)} %get-tuple-element.20), kind=kOutput, calls=%fused_computation.8 | convolution fusion | flops 1391026176 | bytes 14524416 | tf_op jit(solution)/shard_map/mycj,ycko->mokj/dot_general | solution.py:83
  71.6 28.5 %copy.83 = bf16[384,2,96,49]{0,1,3,2:T(2,128)(2,1)} copy(bf16[384,2,96,49]{0,2,3,1:T(8,128)(2,1)} %fusion.2) | data formatting | bytes 14450688 | tf_op jit(solution)/shard_map/convert_element_type | solution.py:85
  100.2 11.8 %gather_fusion.1 = bf16[1536,384,2]{1,2,0:T(2,128)(2,1)S(1)} fusion(bf16[384,2,96,49]{0,1,3,2:T(2,128)(2,1)} %copy.83, s32[1536]{0:T(1024)S(1)} %fusion.48), kind=kCustom, calls=%fused_computation.1 | custom fusion | bytes 4730880 | tf_op jit(solution)/shard_map/gather | solution.py:86
  112.0 4.8 %fusion.70 = (bf16[384,1,1536]{0,1,2:T(2,128)(2,1)}, bf16[384,1,1536]{0,1,2:T(2,128)(2,1)}) fusion(bf16[384,2,1536]{0,1,2:T(2,128)(2,1)S(1)} %bitcast.117), kind=kLoop, calls=%fused_computation.111 | loop fusion | bytes 4718592 | tf_op jit(solution)/shard_map/slice | solution.py:87
  116.9 5.5 %copy.84 = bf16[384,1,1536]{2,0,1:T(8,128)(2,1)S(1)} copy(bf16[384,1,1536]{0,1,2:T(2,128)(2,1)} %get-tuple-element.18) | data formatting | bytes 2359296 | tf_op jit(solution)/shard_map/slice | solution.py:87
  124.6 4.8 %copy.85 = bf16[16,1,64,6,96]{2,0,4,3,1:T(8,128)(2,1)S(1)} copy(bf16[16,1,64,6,96]{4,0,3,2,1:T(8,128)(2,1)} %bitcast.128) | data formatting | bytes 2359296 | tf_op jit(solution)/shard_map/transpose | solution.py:19
  130.4 3.3 copy.115
  133.6 5.8 %reshape.322 = bf16[256,2,1152]{2,1,0:T(2,128)(2,1)} reshape(bf16[256,1,6,6,64]{4,3,2,1,0:T(8,128)(2,1)} %bitcast.118) | data formatting | bytes 2359296
  139.4 15.6 %all-to-all-start = ((bf16[256,2,1152]{2,1,0:T(2,128)(2,1)}), bf16[256,2,1152]{2,1,0:T(2,128)(2,1)}, u32[]{:S(2)}, u32[]{:S(2)}) async-start(bf16[256,2,1152]{2,1,0:T(2,128)(2,1)} %reshape.322), calls=%async_computation | async-start | bytes 2359296 | tf_op jit(solution)/shard_map/all_to_all | solution.py:34
  155.0 4.9 %copy.90 = bf16[384,1,1536]{2,0,1:T(8,128)(2,1)} copy(bf16[384,1,1536]{0,1,2:T(2,128)(2,1)S(1)} %copy-done.3) | data formatting | bytes 2359296 | tf_op jit(solution)/shard_map/slice | solution.py:88
  159.9 3.8 %reshape_stack_reshape_squeeze.7 = bf16[1,64,6,16,96]{4,3,2,1,0:T(8,128)(2,1)} reshape(bf16[384,1,1536]{2,0,1:T(8,128)(2,1)} %copy.90) | data formatting | bytes 2359296 | tf_op jit(solution)/shard_map/reshape;stack;reshape;squeeze | solution.py:18
  163.7 4.4 %copy.91 = bf16[16,1,64,6,96]{2,0,4,3,1:T(8,128)(2,1)S(1)} copy(bf16[16,1,64,6,96]{4,0,3,2,1:T(8,128)(2,1)} %bitcast.129) | data formatting | bytes 2359296 | tf_op jit(solution)/shard_map/transpose | solution.py:19
  169.1 3.3 copy.114
  172.4 5.7 %reshape.320 = bf16[256,2,1152]{2,1,0:T(2,128)(2,1)} reshape(bf16[256,1,6,6,64]{4,3,2,1,0:T(8,128)(2,1)} %bitcast.119) | data formatting | bytes 2359296
  178.1 9.1 %all-to-all-done = bf16[256,2,1152]{2,1,0:T(2,128)(2,1)} async-done(((bf16[256,2,1152]{2,1,0:T(2,128)(2,1)}), bf16[256,2,1152]{2,1,0:T(2,128)(2,1)}, u32[]{:S(2)}, u32[]{:S(2)}) %all-to-all-start) | async-done | bytes 1179680 | tf_op jit(solution)/shard_map/all_to_all | solution.py:34
  187.1 7.3 %all-to-all-start.1 = ((bf16[256,2,1152]{2,1,0:T(2,128)(2,1)}), bf16[256,2,1152]{2,1,0:T(2,128)(2,1)S(1)}, u32[]{:S(2)}, u32[]{:S(2)}) async-start(bf16[256,2,1152]{2,1,0:T(2,128)(2,1)} %reshape.320), calls=%async_computation.1 | async-start | bytes 2359296 | tf_op jit(solution)/shard_map/all_to_all | solution.py:34
  197.5 5.5 %reshape.323 = bf16[256,1,6,6,64]{4,3,2,1,0:T(8,128)(2,1)} reshape(bf16[256,2,1152]{2,1,0:T(2,128)(2,1)} %all-to-all-done) | data formatting | bytes 2359296
  207.3 3.5 %reshape_transpose_reshape.6 = bf16[1,1024,96,6]{1,2,3,0:T(8,128)(2,1)S(1)} reshape(bf16[16,1,64,16,6,6]{2,0,4,3,5,1:T(8,128)(2,1)} %copy.89) | data formatting | bytes 2359296 | tf_op jit(solution)/shard_map/reshape;transpose;reshape | solution.py:25
  210.7 16.5 %all-to-all-done.1 = bf16[256,2,1152]{2,1,0:T(2,128)(2,1)S(1)} async-done(((bf16[256,2,1152]{2,1,0:T(2,128)(2,1)}), bf16[256,2,1152]{2,1,0:T(2,128)(2,1)S(1)}, u32[]{:S(2)}, u32[]{:S(2)}) %all-to-all-start.1) | async-done | bytes 1179680 | tf_op jit(solution)/shard_map/all_to_all | solution.py:34
  227.3 3.1 reshape.321
  234.7 3.5 %reshape_transpose_reshape.7 = bf16[1,1024,96,6]{1,2,3,0:T(8,128)(2,1)S(1)} reshape(bf16[16,1,64,16,6,6]{2,0,4,3,5,1:T(8,128)(2,1)} %copy.95) | data formatting | bytes 2359296 | tf_op jit(solution)/shard_map/reshape;transpose;reshape | solution.py:25
  248.3 2.9 concatenate.24
  252.5 4.8 %copy.98 = bf16[1,16,64,576]{3,2,1,0:T(8,128)(2,1)} copy(bf16[1,16,64,576]{2,1,3,0:T(8,128)(2,1)} %concatenate.23) | data formatting | bytes 2359296 | tf_op jit(solution)/shard_map/concatenate | solution.py:142
  257.3 3.8 %copy.99 = bf16[1,16,64,576]{3,2,1,0:T(8,128)(2,1)} copy(bf16[1,16,64,576]{2,1,3,0:T(8,128)(2,1)S(1)} %copy-done.2) | data formatting | bytes 2359296 | tf_op jit(solution)/shard_map/concatenate | solution.py:142
  268.2 2.9 subtract_multiply_fusion
  271.0 55.8 %all_to_all.20 = f32[16,64,1024]{2,1,0:T(8,128)} all-to-all(f32[16,64,1024]{2,1,0:T(8,128)S(1)} %bitcast.130), channel_id=1, replica_groups=mesh['fft'=16,'pair'=16] {'pair'}, dimensions={0} | all-to-all | bytes 8388608 | tf_op jit(solution)/shard_map/all_to_all | solution.py:41
  330.1 14.6 %all_to_all.21 = f32[16,1,4096]{2,1,0:T(1,128)S(1)} all-to-all(f32[16,1,4096]{2,1,0:T(1,128)S(1)} %reshape.324), channel_id=1, replica_groups=mesh['fft'=16,'pair'=16] {'fft'}, dimensions={0} | all-to-all | bytes 524288 | tf_op jit(solution)/shard_map/all_to_all | solution.py:41
  (65 shorter events, 39.7 us)
Async XLA Ops:
  0.0 1.2 copy-start
  71.6 28.6 %copy-start.6 = (s32[1536]{0:T(1024)S(1)}, s32[1536]{0:T(1024)}, u32[]{:S(2)}) copy-start(s32[1536]{0:T(1024)} %param.14) | copy-start | bytes 18436
  133.6 21.4 %copy-start.3 = (bf16[384,1,1536]{0,1,2:T(2,128)(2,1)S(1)}, bf16[384,1,1536]{0,1,2:T(2,128)(2,1)}, u32[]{:S(2)}) copy-start(bf16[384,1,1536]{0,1,2:T(2,128)(2,1)} %get-tuple-element.19) | copy-start | bytes 3538948
  139.4 47.7 %all-to-all-start = ((bf16[256,2,1152]{2,1,0:T(2,128)(2,1)}), bf16[256,2,1152]{2,1,0:T(2,128)(2,1)}, u32[]{:S(2)}, u32[]{:S(2)}) async-start(bf16[256,2,1152]{2,1,0:T(2,128)(2,1)} %reshape.322), calls=%async_computation | async-start | bytes 2359296 | tf_op jit(solution)/shard_map/all_to_all | solution.py:34
  172.4 22.7 %copy-start.7 = (f32[1024]{0:T(1024)S(1)}, f32[1024]{0:T(1024)}, u32[]{:S(2)}) copy-start(f32[1024]{0:T(1024)} %param.12) | copy-start | bytes 12292
  172.4 22.8 %copy-start.8 = (s32[16]{0:T(128)S(1)}, s32[16]{0:T(128)}, u32[]{:S(2)}) copy-start(s32[16]{0:T(128)} %param.15) | copy-start | bytes 196
  172.4 23.6 %copy-start.9 = (f32[8]{0:T(128)S(1)}, f32[8]{0:T(128)}, u32[]{:S(2)}) copy-start(f32[8]{0:T(128)} %param.11) | copy-start | bytes 100
  187.1 40.2 %all-to-all-start.1 = ((bf16[256,2,1152]{2,1,0:T(2,128)(2,1)}), bf16[256,2,1152]{2,1,0:T(2,128)(2,1)S(1)}, u32[]{:S(2)}, u32[]{:S(2)}) async-start(bf16[256,2,1152]{2,1,0:T(2,128)(2,1)} %reshape.320), calls=%async_computation.1 | async-start | bytes 2359296 | tf_op jit(solution)/shard_map/all_to_all | solution.py:34
  252.5 4.8 %copy-start.2 = (bf16[1,16,64,576]{2,1,3,0:T(8,128)(2,1)S(1)}, bf16[1,16,64,576]{2,1,3,0:T(8,128)(2,1)}, u32[]{:S(2)}) copy-start(bf16[1,16,64,576]{2,1,3,0:T(8,128)(2,1)} %concatenate.24) | copy-start | bytes 3538948
  265.8 2.1 copy-start.4
  265.8 2.3 copy-start.5
  326.8 20.4 %copy-start.1 = (bf16[8,6,9216]{2,0,1:T(8,128)(2,1)S(1)}, bf16[8,6,9216]{2,0,1:T(8,128)(2,1)}, u32[]{:S(2)}) copy-start(bf16[8,6,9216]{2,0,1:T(8,128)(2,1)} %param.9) | copy-start | bytes 2654212
where the time goes:
time: 355 us; the launch traced here: 348 us
  local copies, waits for them, and re-layouts  182 us (51%)
  blocking collectives  70.4 us (20%)
  waiting for transfers between devices  25.6 us (7%)
  matrix products  24.7 us (7%)
  starting transfers between devices  22.8 us (6%)
  other arithmetic  19.4 us (5%)
    all_to_all x2, blocking collectives, sent_and_summed(): lax.all_to_all(blocks, axis, split_axis=0, concat_axis=0, tiled=True)  70.4 us
    convert_element_type x1, local copies, waits for them, and re-layouts, plane_coefficients(): transformed = jnp.einsum('mycj,ycko->mokj', z_coeffs, plane_table, prefer...  28.5 us
    all_to_all x2, waiting for transfers between devices, one_exchange(): lax.all_to_all(blocks, axis, split_axis=0, concat_axis=0, tiled=True)  25.6 us
    all_to_all x2, starting transfers between devices, one_exchange(): lax.all_to_all(blocks, axis, split_axis=0, concat_axis=0, tiled=True)  22.8 us
    unnamed x26, local copies, waits for them, and re-layouts  20.9 us
    reshape x1, local copies, waits for them, and re-layouts, plane_coefficients(): density.reshape(bands * planes * G, G)  16.7 us
    reshape x1, local copies, waits for them, and re-layouts, plane_coefficients(): z_coeffs = z_coeffs.astype(jnp.bfloat16).reshape(bands * planes, G, 2, KZ)  15 us
    concatenate x4, local copies, waits for them, and re-layouts, body(): joined = jnp.concatenate([flat_re, flat_im], axis=2)  14.3 us
  transfers between devices with their start and end apart: 2, of which 2 were waited for; matrix products, arithmetic and copies ran while one was open for 11% of the time, Pallas kernels for 0%

commit v1 on v0

v1 whole, which is shorter than its diff:
```python
import math

import jax
import jax.numpy as jnp
import numpy as np
from jax import lax
from jax.experimental import pallas as pl
from jax.experimental.pallas import tpu as pltpu
from jax.sharding import PartitionSpec as P

G = 96
R = 24
KZ = 49
NPEN = 1536
NBAND = 1024
FFT = 16
PAIR = 16
BANDS = NBAND // PAIR
PLANES = G // FFT
PENS = NPEN // (FFT * PAIR)
ROWS = 40
STEP = 16
NJ = R + 1


def rounded_tables():
    turns = (np.arange(G)[:, None] * np.arange(G)[None, :]) % G
    angle = turns.astype(np.float32) * np.float32(2.0 * math.pi / G)
    return np.cos(angle), np.sin(angle)


def z_stage_table():
    cos, sin = rounded_tables()
    table = np.zeros((NJ, 2, 8, 8, G), np.float32)
    for y in range(8):
        table[:, 0, y, y] = cos[:NJ]
        table[:, 1, y, y] = -sin[:NJ]
    return table.reshape(NJ * 2 * 8, 8 * G)


def y_stage_table():
    cos, sin = rounded_tables()
    return np.block([[cos, sin], [-sin, cos]])


def x_stage_table():
    cos, sin = rounded_tables()
    table = np.zeros((2, G, 2, FFT, ROWS), np.float32)
    for low in range(2):
        for source in range(FFT):
            for pencil in range(PENS):
                for high in range(3):
                    x = source * PLANES + 2 * high + low
                    for part in range(2):
                        row = pencil * 6 + part * 3 + high
                        if part == 0:
                            table[0, :, low, source, row] = cos[x]
                            table[1, :, low, source, row] = -sin[x]
                        else:
                            table[0, :, low, source, row] = sin[x]
                            table[1, :, low, source, row] = cos[x]
    return table.reshape(2 * G, 2 * FFT * ROWS)


def plane_kernel(occ_index, slots, virtual, occupied, z_table, y_table, out, z_parts, coeffs):
    step = pl.program_id(0)
    chosen = lax.broadcasted_iota(jnp.int32, (PLANES, 8, STEP * G), 1) == occ_index[0]
    orbital = jnp.sum(
        jnp.where(chosen, occupied[...].astype(jnp.float32), 0.0), axis=1, keepdims=True
    )
    pieces = []
    for half in range(2):
        lanes = slice(half * 8 * G, (half + 1) * 8 * G)
        density = (virtual[:, :, lanes].astype(jnp.float32) * orbital[:, :, lanes]).astype(
            jnp.bfloat16
        )
        density = density.reshape(PLANES * BANDS, 8 * G)
        z_coeffs = lax.dot_general(
            z_table[...], density, (((1,), (1,)), ((), ())), preferred_element_type=jnp.float32
        )
        pieces.append(z_coeffs.reshape(NJ * 2, 8, PLANES * BANDS))
    z_parts[:, pl.ds(pl.multiple_of(step * STEP, STEP), STEP), :] = jnp.concatenate(
        pieces, axis=1
    ).astype(jnp.bfloat16)

    @pl.when(step == pl.num_programs(0) - 1)
    def _():
        def one_frequency(j, carry):
            both = z_parts[pl.ds(2 * j, 2)].reshape(2 * G, PLANES * BANDS)
            values = jnp.dot(y_table[...], both, preferred_element_type=jnp.float32)
            for part in range(2):
                for high in range(3):
                    coeffs[pl.ds(j * (G * 8) + part * 3 + high, G, stride=8), :] = values[
                        part * G : (part + 1) * G, high * 128 : (high + 1) * 128
                    ]
            return carry

        lax.fori_loop(0, NJ, one_frequency, 0)

        def one_target(target, carry):
            rows = []
            for pencil in range(PENS):
                slot = slots[target * PENS + pencil]
                rows.append(coeffs[pl.ds(pl.multiple_of(slot * 8, 8), 8), :][:6])
            rows.append(jnp.zeros((ROWS - 6 * PENS, 128), jnp.float32))
            out[target] = jnp.concatenate(rows, axis=0).astype(jnp.bfloat16)
            return carry

        lax.fori_loop(0, FFT * PAIR, one_target, 0, unroll=4)


def plane_chunks(virtual, occupied, occ_index, slots):
    return pl.pallas_call(
        plane_kernel,
        grid_spec=pltpu.PrefetchScalarGridSpec(
            num_scalar_prefetch=2,
            grid=(G // STEP,),
            in_specs=[
                pl.BlockSpec((PLANES, BANDS, STEP * G), lambda s, *_: (0, 0, s)),
                pl.BlockSpec((PLANES, 8, STEP * G), lambda s, *_: (0, 0, s)),
                pl.BlockSpec((NJ * 16, 8 * G), lambda s, *_: (0, 0)),
                pl.BlockSpec((2 * G, 2 * G), lambda s, *_: (0, 0)),
            ],
            out_specs=pl.BlockSpec((FFT * PAIR, ROWS, 128), lambda s, *_: (0, 0, 0)),
            scratch_shapes=[
                pltpu.VMEM((NJ * 2, G, PLANES * BANDS), jnp.bfloat16),
                pltpu.VMEM((NJ * G * 8, 128), jnp.float32),
            ],
        ),
        out_shape=jax.ShapeDtypeStruct((FFT * PAIR, ROWS, 128), jnp.bfloat16),
        compiler_params=pltpu.CompilerParams(vmem_limit_bytes=56 * 1024 * 1024),
        name="planes",
    )(
        occ_index,
        slots,
        virtual,
        occupied,
        jnp.asarray(z_stage_table(), jnp.bfloat16),
        jnp.asarray(y_stage_table(), jnp.bfloat16),
    )


def swap_halves(first, second, low):
    left = jnp.where(low, first, pltpu.roll(second, 64, 1))
    right = jnp.where(low, pltpu.roll(first, 64, 1), second)
    return left, right


def gram_kernel(places, plane_freq, signs, scale, arrived, x_table, mine, theirs, stacked, spectra):
    for pair in range(PAIR // 2):
        first = arrived[:, 2 * pair].astype(jnp.float32).reshape(FFT * ROWS, 128)
        second = arrived[:, 2 * pair + 1].astype(jnp.float32).reshape(FFT * ROWS, 128)
        low = lax.broadcasted_iota(jnp.int32, (FFT * ROWS, 128), 1) < 64
        left, right = swap_halves(first, second, low)
        lanes = slice(pair * 128, (pair + 1) * 128)
        stacked[0 : FFT * ROWS, lanes] = left.astype(jnp.bfloat16)
        stacked[FFT * ROWS :, lanes] = right.astype(jnp.bfloat16)

    freq = lax.broadcasted_iota(jnp.int32, (2 * G, 128), 0) % G
    freq = (freq + G // 2) % G - G // 2
    squared_x = freq * freq
    exponent = jnp.full((2 * G, 128), scale[0], jnp.float32)
    norm = exponent * G
    norm = norm * jnp.sqrt(norm)
    column = lax.broadcasted_iota(jnp.int32, (2 * G, 2 * FFT * ROWS), 1) % ROWS
    for pencil in range(PENS):
        squared = (squared_x + plane_freq[pencil]).astype(jnp.float32)
        weight = 1.0 / (norm * (1.0 + squared / (exponent * exponent)))
        sign = signs[pencil]
        factor = jnp.where(
            column // 3 == 2 * pencil,
            1.0,
            jnp.where(column // 3 == 2 * pencil + 1, sign, 0.0),
        ).astype(jnp.bfloat16)
        values = jnp.dot(x_table[...] * factor, stacked[...], preferred_element_type=jnp.float32)
        weight = jnp.concatenate([weight] * (NBAND // 128), axis=1)
        spectra[pencil * 2 * G : (pencil + 1) * 2 * G, :] = (values * weight).astype(jnp.bfloat16)

    low = lax.broadcasted_iota(jnp.int32, (BANDS // 2, 128), 1) < 64
    for group in range(4):
        gram = lax.dot_general(
            spectra[:, group * 256 : (group + 1) * 256],
            spectra[...],
            (((0,), (0,)), ((), ())),
            preferred_element_type=jnp.float32,
        )
        for inner in range(4):
            place = places[group * 4 + inner]
            parts = []
            for pair in range(PAIR // 2):
                tile = gram[inner * 64 : (inner + 1) * 64, pair * 128 : (pair + 1) * 128]
                parts.extend(swap_halves(tile[:32], tile[32:], low))

            @pl.when(place < PAIR // 2)
            def _():
                for part in range(PAIR):
                    mine[place, part] = parts[part]

            @pl.when(place >= PAIR // 2)
            def _():
                for part in range(PAIR):
                    theirs[place - PAIR // 2, part] = parts[part]


def gram_halves(places, plane_freq, signs, scale, arrived):
    half = jax.ShapeDtypeStruct((PAIR // 2, PAIR, 32, 128), jnp.float32)
    smem = pl.BlockSpec(memory_space=pltpu.SMEM)
    vmem = pl.BlockSpec(memory_space=pltpu.VMEM)
    return pl.pallas_call(
        gram_kernel,
        in_specs=[smem, smem, smem, smem, vmem, vmem],
        out_specs=[vmem, vmem],
        out_shape=[half, half],
        scratch_shapes=[
            pltpu.VMEM((2 * FFT * ROWS, NBAND), jnp.bfloat16),
            pltpu.VMEM((PENS * 2 * G, NBAND), jnp.bfloat16),
        ],
        compiler_params=pltpu.CompilerParams(vmem_limit_bytes=56 * 1024 * 1024),
        name="gram",
    )(
        places,
        plane_freq,
        signs,
        scale,
        arrived.reshape(FFT, PAIR, ROWS, 128),
        jnp.asarray(x_stage_table(), jnp.bfloat16),
    )


def body(
    virt_orbitals,
    occ_orbitals,
    occ_index,
    occ_energy,
    band_energy,
    geminal_exponent,
    pencil_index,
    block_owner,
):
    fft_at = lax.axis_index("fft")
    pair_at = lax.axis_index("pair")
    k = pencil_index // KZ
    j = pencil_index % KZ - R
    slots = jnp.abs(j) * G + jnp.where(j >= 0, k, (G - k) % G)
    chunks = plane_chunks(
        jnp.transpose(virt_orbitals, (1, 0, 2)),
        jnp.transpose(occ_orbitals, (1, 0, 2)),
        occ_index,
        slots,
    )
    arrived = lax.all_to_all(chunks, ("fft", "pair"), split_axis=0, concat_axis=0, tiled=True)

    start = (fft_at * PAIR + pair_at) * PENS
    kept = lax.dynamic_slice_in_dim(pencil_index, start, PENS)
    freq_y = (kept // KZ + G // 2) % G - G // 2
    freq_z = kept % KZ - R
    signs = jnp.where(freq_z >= 0, 1.0, -1.0).astype(jnp.float32)
    order = jnp.arange(PAIR, dtype=jnp.int32)
    owner = jnp.sum(
        jnp.where(block_owner[:, None] == order[None, :], order[:, None], 0), axis=0
    )
    places = owner // 2 + jnp.where(owner % 2 == pair_at % 2, 0, PAIR // 2)
    mine, theirs = gram_halves(
        places, freq_y * freq_y + freq_z * freq_z, signs, geminal_exponent, arrived
    )
    swapped = lax.ppermute(theirs, "pair", [(i, i ^ 1) for i in range(PAIR)])
    same_core = [list(range(0, PAIR, 2)), list(range(1, PAIR, 2))]
    rows = lax.all_to_all(
        mine + swapped, "pair", 0, 0, tiled=True, axis_index_groups=same_core
    ).sum(axis=0)
    total = lax.all_to_all(rows, "fft", 0, 0, tiled=True).sum(axis=0)
    gram = jnp.concatenate([total[:, :64], total[:, 64:]], axis=0)
    block = lax.dynamic_index_in_dim(block_owner, pair_at, keepdims=False)
    row_energy = lax.dynamic_slice_in_dim(band_energy, block * BANDS, BANDS)
    column_energy = lax.dynamic_slice_in_dim(band_energy, fft_at * BANDS, BANDS)
    occupied_energy = lax.dynamic_index_in_dim(occ_energy, occ_index[0], keepdims=False)
    return (row_energy[:, None] + column_energy[None, :] - 2.0 * occupied_energy) * gram


def solution(mesh):
    return jax.shard_map(
        body,
        mesh=mesh,
        in_specs=(P("pair", "fft", None), P(None, "fft", None), P(), P(), P(), P(), P(), P()),
        out_specs=P("pair", "fft"),
        check_vma=False,
    )
```

time: 355 us -> 168 us (0.47); the launches traced: 348 us -> 168 us
  local copies, waits for them, and re-layouts: 182 us -> 3.59 us
  waiting for transfers between devices: 25.6 us -> 70.3 us
  blocking collectives: 70.4 us -> 31.7 us
  Pallas kernels: 0 us -> 30.4 us
  matrix products: 24.7 us -> 0 us
  other arithmetic: 19.4 us -> 8.29 us
    convert_element_type x4 -> x0, local copies, waits for them, and re-layouts: 41.7 us -> none  [the longest x1 28.5 us: plane_coefficients(): transformed = jnp.einsum('mycj,ycko->mokj', z_coeffs, plane_table, prefer...]
    reshape x8 -> x0, local copies, waits for them, and re-layouts: 41 us -> none  [the longest x1 16.7 us: plane_coefficients(): density.reshape(bands * planes * G, G)]
    all_to_all x2, waiting for transfers between devices: 25.6 us -> 66.3 us  [the longest x1 59.7 us: body(): lax.all_to_all(chunks, ('fft', 'pair'), split_axis=0, concat_axis=0, tile...]
    all_to_all x2 -> x1, blocking collectives: 70.4 us -> 31.7 us  [body(): lax.all_to_all(mine + swapped, 'pair', 0, 0, tiled=True, axis_index_group...]
    pallas_call x0 -> x2, Pallas kernels: none -> 30.4 us  [the longest x1 17.1 us: plane_chunks(): pl.pallas_call(plane_kernel, grid_spec=pltpu.PrefetchScalarGridSpec(num_s...]
    dot_general x5 -> x0, matrix products: 24.7 us -> none  [the longest x1 9.98 us: plane_coefficients(): jnp.dot(density.reshape(bands * planes * G, G), z_table, preferred_elemen...]
    unnamed x26 -> x6, local copies, waits for them, and re-layouts: 20.9 us -> 1.51 us
    gather x4 -> x0, local copies, waits for them, and re-layouts: 15.2 us -> none  [the longest x1 11.8 us: plane_coefficients(): chosen = transformed[:, :, pencils // KZ, pencils % KZ]]
  transfers between devices with their start and end apart: 2 -> 3, of which waited for: 2 -> 3; matrix products, arithmetic and copies ran while one was open for 11% -> 3% of each run, Pallas kernels for 0% -> 0%
where the time goes in v1:
time: 168 us
  waiting for transfers between devices  70.3 us (42%)
  blocking collectives  31.7 us (19%)
  Pallas kernels  30.4 us (18%)
  starting transfers between devices  20.8 us (12%)
  other arithmetic  8.29 us (5%)
  local copies, waits for them, and re-layouts  3.59 us (2%)
  between operations  2.67 us (2%)
    all_to_all x1, waiting for transfers between devices, body(): lax.all_to_all(chunks, ('fft', 'pair'), split_axis=0, concat_axis=0, tile...  59.7 us
    all_to_all x1, blocking collectives, body(): lax.all_to_all(mine + swapped, 'pair', 0, 0, tiled=True, axis_index_group...  31.7 us
    pallas_call x1, Pallas kernels, plane_chunks(): pl.pallas_call(plane_kernel, grid_spec=pltpu.PrefetchScalarGridSpec(num_s...  17.1 us
    all_to_all x1, starting transfers between devices, body(): lax.all_to_all(chunks, ('fft', 'pair'), split_axis=0, concat_axis=0, tile...  14.7 us
    pallas_call x1, Pallas kernels, gram_halves(): pl.pallas_call(gram_kernel, in_specs=[smem, smem, smem, smem, vmem, vmem]...  13.3 us
    all_to_all x1, waiting for transfers between devices, body(): total = lax.all_to_all(rows, 'fft', 0, 0, tiled=True).sum(axis=0)  6.6 us
    all_to_all x1, starting transfers between devices, body(): total = lax.all_to_all(rows, 'fft', 0, 0, tiled=True).sum(axis=0)  5.2 us
    ppermute x1, waiting for transfers between devices, body(): swapped = lax.ppermute(theirs, 'pair', [(i, i ^ 1) for i in range(PAIR)])  4 us
  transfers between devices with their start and end apart: 3, of which 3 were waited for; matrix products, arithmetic and copies ran while one was open for 3% of the time, Pallas kernels for 0%

profile of v1, /device:TPU:2, one launch (start us, length us, event | category | flops | bytes accessed | tf_op | source)
XLA Modules:
  0.0 167.8 jit_solution(6697886298838880533)
XLA Ops:
  0.7 1.3 fusion.2.slots
  2.0 17.1 %planes.1 = bf16[256,40,128]{2,1,0:T(8,128)(2,1)} custom-call(s32[1]{0:T(128)} %copy.12.occ_index, s32[1536]{0:T(1024)} %fusion.2.slots, bf16[6,64,9216]{2,1,0:T(8,128)(2,1)} %bitcast.10, bf16[6,8,9216]{2,1,0:T(8,128)(2,1)} %bitcast.11, bf16[400,768]{1,0:T(8,128)(2,1)} %constant.128.clone.z_table, bf16[192,192]{1,0:T(8,128)(2,1)} %constant.129.clone.y_table), custom_call_target="tpu_custom_call" | custom-call | tf_op jit(solution)/shard_map/planes/pallas_call | solution.py:113
  19.1 0.0 copy-start.1
  19.1 14.7 %all-to-all-start = ((bf16[256,40,128]{2,1,0:T(8,128)(2,1)}), bf16[256,40,128]{2,1,0:T(8,128)(2,1)S(1)}, u32[]{:S(2)}, u32[]{:S(2)}) async-start(bf16[256,40,128]{2,1,0:T(8,128)(2,1)} %planes.1), calls=%async_computation | async-start | bytes 5242880 | tf_op jit(solution)/shard_map/all_to_all | solution.py:251
  34.5 1.3 compare_select_fusion
  35.8 0.0 copy-done.1
  35.8 0.1 select_reduce_fusion
  35.9 1.4 fusion.10.plane_freq
  37.2 0.5 fusion.7.places
  37.8 59.7 %all-to-all-done = bf16[256,40,128]{2,1,0:T(8,128)(2,1)S(1)} async-done(((bf16[256,40,128]{2,1,0:T(8,128)(2,1)}), bf16[256,40,128]{2,1,0:T(8,128)(2,1)S(1)}, u32[]{:S(2)}, u32[]{:S(2)}) %all-to-all-start) | async-done | bytes 2621472 | tf_op jit(solution)/shard_map/all_to_all | solution.py:251
  97.5 0.0 copy-start
  97.5 1.5 copy-done
  99.0 13.3 %gram.1 = (f32[8,16,32,128]{3,2,1,0:T(8,128)}, f32[8,16,32,128]{3,2,1,0:T(8,128)}) custom-call(s32[16]{0:T(128)} %fusion.7.places, s32[6]{0:T(128)} %fusion.10.plane_freq, f32[6]{0:T(128)} %get-tuple-element.9.signs, f32[1]{0:T(128)S(6)} %copy.13.scale, bf16[16,16,40,128]{3,2,1,0:T(8,128)(2,1)} %bitcast.9, bf16[192,1280]{1,0:T(8,128)(2,1)} %constant.130.clone.x_table), custom_call_target="tpu_custom_call" | custom-call | tf_op jit(solution)/shard_map/gram/pallas_call | solution.py:209
  112.3 0.9 collective-permute-start
  113.2 4.0 %collective-permute-done = f32[8,16,32,128]{3,2,1,0:T(8,128)S(1)} collective-permute-done((f32[8,16,32,128]{3,2,1,0:T(8,128)}, f32[8,16,32,128]{3,2,1,0:T(8,128)S(1)}, u32[]{:S(2)}, u32[]{:S(2)}) %collective-permute-start) | collective-permute-done | bytes 2097184 | tf_op jit(solution)/shard_map/ppermute | solution.py:266
  117.2 2.1 %add.103 = f32[8,16,32,128]{3,2,1,0:T(8,128)S(1)} add(f32[8,16,32,128]{3,2,1,0:T(8,128)} %get-tuple-element.7, f32[8,16,32,128]{3,2,1,0:T(8,128)S(1)} %collective-permute-done) | non-fusion elementwise | flops 524288 | bytes 6291456 | tf_op jit(solution)/shard_map/add | solution.py:269
  119.3 31.7 %all_to_all.15 = f32[8,16,32,128]{3,2,1,0:T(8,128)S(1)} all-to-all(f32[8,16,32,128]{3,2,1,0:T(8,128)S(1)} %add.103), channel_id=1, replica_groups={{0,2,4,6,8,10,12,14},{1,3,5,7,9,11,13,15},{16,18,20,22,24,26,28,30},{17..., dimensions={0} | all-to-all | bytes 4194304 | tf_op jit(solution)/shard_map/all_to_all | solution.py:268
  151.0 0.0 copy-start.2
  151.0 0.9 reduce_sum.28
  151.9 5.2 %all-to-all-start.2 = ((f32[16,32,128]{2,1,0:T(8,128)}), f32[16,32,128]{2,1,0:T(8,128)S(1)}, u32[]{:S(2)}, u32[]{:S(2)}) async-start(f32[16,32,128]{2,1,0:T(8,128)} %reduce_sum.28), calls=%async_computation.2 | async-start | bytes 524288 | tf_op jit(solution)/shard_map/all_to_all | solution.py:271
  157.1 0.6 dynamic_slice.17
  158.3 0.0 copy-done.2
  158.3 0.6 dynamic_slice.20
  159.6 0.8 fusion.14
  160.4 6.6 %all-to-all-done.2 = f32[16,32,128]{2,1,0:T(8,128)S(1)} async-done(((f32[16,32,128]{2,1,0:T(8,128)}), f32[16,32,128]{2,1,0:T(8,128)S(1)}, u32[]{:S(2)}, u32[]{:S(2)}) %all-to-all-start.2) | async-done | bytes 262176 | tf_op jit(solution)/shard_map/all_to_all | solution.py:271
  167.1 0.1 fusion.13
  167.1 0.7 maximum_multiply_fusion
  (1 shorter events, 0.0 us)
Async XLA Ops:
  19.1 16.7 %copy-start.1 = (s32[16]{0:T(128)S(1)}, s32[16]{0:T(128)}, u32[]{:S(2)}) copy-start(s32[16]{0:T(128)} %param.18) | copy-start | bytes 196
  19.1 78.4 %all-to-all-start = ((bf16[256,40,128]{2,1,0:T(8,128)(2,1)}), bf16[256,40,128]{2,1,0:T(8,128)(2,1)S(1)}, u32[]{:S(2)}, u32[]{:S(2)}) async-start(bf16[256,40,128]{2,1,0:T(8,128)(2,1)} %planes.1), calls=%async_computation | async-start | bytes 5242880 | tf_op jit(solution)/shard_map/all_to_all | solution.py:251
  97.5 1.5 copy-start
  112.3 4.9 %collective-permute-start = (f32[8,16,32,128]{3,2,1,0:T(8,128)}, f32[8,16,32,128]{3,2,1,0:T(8,128)S(1)}, u32[]{:S(2)}, u32[]{:S(2)}) collective-permute-start(f32[8,16,32,128]{3,2,1,0:T(8,128)} %get-tuple-element.8), channel_id=1, source_target_pairs={{0,1},{1,0},{2,3},{3,2},{4,5},{5,4},{6,7},{7,6},{8,9},{9,8},{10,11... | collective-permute-start | bytes 6291464 | tf_op jit(solution)/shard_map/ppermute | solution.py:266
  151.0 7.4 %copy-start.2 = (f32[8]{0:T(128)S(1)}, f32[8]{0:T(128)}, u32[]{:S(2)}) copy-start(f32[8]{0:T(128)} %param.14) | copy-start | bytes 100
  151.9 15.1 %all-to-all-start.2 = ((f32[16,32,128]{2,1,0:T(8,128)}), f32[16,32,128]{2,1,0:T(8,128)S(1)}, u32[]{:S(2)}, u32[]{:S(2)}) async-start(f32[16,32,128]{2,1,0:T(8,128)} %reduce_sum.28), calls=%async_computation.2 | async-start | bytes 524288 | tf_op jit(solution)/shard_map/all_to_all | solution.py:271

commit v2 on v1

v2 whole, which is shorter than its diff:
```python
import math

import jax
import jax.numpy as jnp
import numpy as np
from jax import lax
from jax.experimental import pallas as pl
from jax.experimental.pallas import tpu as pltpu
from jax.sharding import PartitionSpec as P

G = 96
R = 24
KZ = 49
NPEN = 1536
NBAND = 1024
FFT = 16
PAIR = 16
BANDS = NBAND // PAIR
PLANES = G // FFT
FIRST = 4
SECOND = NPEN // (FFT * PAIR) - FIRST
DEVICES = FFT * PAIR
FIRST_ROWS = 6 * FIRST
SECOND_ROWS = 16
STEP = 16
NJ = R + 1
POINTS = PLANES * BANDS


def rounded_tables():
    turns = (np.arange(G)[:, None] * np.arange(G)[None, :]) % G
    angle = turns.astype(np.float32) * np.float32(2.0 * math.pi / G)
    return np.cos(angle), np.sin(angle)


def z_stage_tables():
    cos, sin = rounded_tables()
    table = np.zeros((2, NJ, 2, 4, 4, G), np.float32)
    for y in range(4):
        for odd in range(2):
            table[odd, :, odd, y, y] = cos[:NJ]
            table[odd, :, 1 - odd, y, y] = -sin[:NJ]
    return table.reshape(2, NJ * 8, 4 * G)


def y_stage_table():
    cos, sin = rounded_tables()
    swapped = np.arange(G).reshape(-1, 2, 4)[:, ::-1].reshape(-1)
    return np.block([[cos, sin[:, swapped]], [-sin, cos[:, swapped]]])


def x_stage_table(pencils, rows):
    cos, sin = rounded_tables()
    table = np.zeros((2, G, 2, FFT, rows), np.float32)
    for low in range(2):
        for source in range(FFT):
            for pencil in range(pencils):
                for high in range(3):
                    x = source * PLANES + 2 * high + low
                    row = pencil * 6 + high
                    table[0, :, low, source, row] = cos[x]
                    table[1, :, low, source, row] = -sin[x]
                    table[0, :, low, source, row + 3] = sin[x]
                    table[1, :, low, source, row + 3] = cos[x]
    return table.reshape(2 * G, 2 * FFT * rows)


def plan_kernel(pencils, slots, weights, squares, total):
    index = pencils[...]
    k = index // KZ
    j = index % KZ - R
    mirror = (G - k) % G
    folded = jnp.where(j > 0, k, jnp.where(j < 0, mirror, jnp.minimum(k, mirror)))
    k_rows = lax.broadcasted_iota(jnp.int32, (G, NPEN), 0)
    j_rows = lax.broadcasted_iota(jnp.int32, (32, NPEN), 0)
    k_hot = jnp.where(k_rows == folded, 1.0, 0.0).astype(jnp.bfloat16)
    j_hot = jnp.where(j_rows == jnp.abs(j), 1.0, 0.0).astype(jnp.bfloat16)
    contract_lanes = (((1,), (1,)), ((), ()))
    contract_rows = (((0,), (0,)), ((), ()))
    count = lax.dot_general(j_hot, k_hot, contract_lanes, preferred_element_type=jnp.float32)
    present = jnp.where(count > 0.5, 1.0, 0.0).astype(jnp.bfloat16)
    upto = jnp.where(
        lax.broadcasted_iota(jnp.int32, (G, G), 0) <= lax.broadcasted_iota(jnp.int32, (G, G), 1),
        1.0,
        0.0,
    ).astype(jnp.bfloat16)
    within = jnp.dot(present, upto, preferred_element_type=jnp.float32)
    before = jnp.where(
        lax.broadcasted_iota(jnp.int32, (32, 32), 1) < lax.broadcasted_iota(jnp.int32, (32, 32), 0),
        1.0,
        0.0,
    ).astype(jnp.bfloat16)
    column_total = within[:, G - 1 : G]
    column_wide = jnp.broadcast_to(column_total, (32, 128))
    start = jnp.dot(before, column_wide.astype(jnp.bfloat16), preferred_element_type=jnp.float32)
    start = start[:, 0:1]
    stop = start + column_total
    entry = lax.broadcasted_iota(jnp.int32, (1, NPEN), 1).astype(jnp.float32)
    past = entry >= stop
    column = jnp.sum(jnp.where(past, 1, 0), axis=0, keepdims=True)
    offset = jnp.sum(jnp.where(past, column_total, 0.0), axis=0, keepdims=True)
    own_column = jnp.where(j_rows == column, 1.0, 0.0).astype(jnp.bfloat16)
    own_within = lax.dot_general(
        within.astype(jnp.bfloat16), own_column, contract_rows, preferred_element_type=jnp.float32
    )
    own_count = lax.dot_general(
        count.astype(jnp.bfloat16), own_column, contract_rows, preferred_element_type=jnp.float32
    )
    row = jnp.sum(jnp.where(own_within <= entry - offset, 1, 0), axis=0, keepdims=True)
    weight = jnp.sum(jnp.where(k_rows == row, own_count, 0.0), axis=0, keepdims=True)
    valid = column < NJ
    row = jnp.minimum(row, G - 1)
    column = jnp.minimum(column, NJ - 1)
    signed = (row + G // 2) % G - G // 2
    slots[...] = jnp.where(valid, column * G + row, 0)
    weights[...] = jnp.where(valid, weight, 0.0)
    squares[...] = jnp.where(valid, signed * signed + column * column, 0)
    total[...] = jnp.broadcast_to(jnp.sum(column_total, axis=0, keepdims=True), (1, 128)).astype(jnp.int32)


def pencil_plan(pencil_index):
    vmem = pl.BlockSpec(memory_space=pltpu.VMEM)
    return pl.pallas_call(
        plan_kernel,
        in_specs=[vmem],
        out_specs=[vmem] * 4,
        out_shape=[
            jax.ShapeDtypeStruct((1, NPEN), jnp.int32),
            jax.ShapeDtypeStruct((1, NPEN), jnp.float32),
            jax.ShapeDtypeStruct((1, NPEN), jnp.int32),
            jax.ShapeDtypeStruct((1, 128), jnp.int32),
        ],
        name="plan",
    )(pencil_index.reshape(1, NPEN))


def plane_kernel(
    occ_index, slots, total, virtual, occupied, z_tables, y_table, out, more, z_parts, coeffs
):
    step = pl.program_id(0)
    chosen = lax.broadcasted_iota(jnp.int32, (PLANES, 8, STEP * G), 1) == occ_index[0]
    orbital = jnp.sum(
        jnp.where(chosen, occupied[...].astype(jnp.float32), 0.0), axis=1, keepdims=True
    )

    def density(group):
        lanes = slice(group * 4 * G, (group + 1) * 4 * G)
        product = virtual[:, :, lanes].astype(jnp.float32) * orbital[:, :, lanes]
        return product.astype(jnp.bfloat16).reshape(POINTS, 4 * G)

    halves = []
    for odd in range(2):
        halves.append(
            lax.dot_general(
                z_tables[odd],
                jnp.concatenate([density(odd), density(odd + 2)], axis=0),
                (((1,), (1,)), ((), ())),
                preferred_element_type=jnp.float32,
            ).reshape(NJ, 8, 2 * POINTS)
        )
    top = lax.broadcasted_iota(jnp.int32, (NJ, 8, POINTS), 1) < 4
    tiles = [[], []]
    for group in range(2):
        lanes = slice(group * POINTS, (group + 1) * POINTS)
        even, odd = halves[0][:, :, lanes], halves[1][:, :, lanes]
        tiles[0].append(jnp.where(top, even, odd))
        tiles[1].append(jnp.where(top, odd, even))
    here = pl.ds(pl.multiple_of(step * STEP, STEP), STEP)
    for part in range(2):
        z_parts[:, part, here, :] = jnp.concatenate(tiles[part], axis=1).astype(jnp.bfloat16)

    @pl.when(step == pl.num_programs(0) - 1)
    def _():
        def transform(j, width):
            both = [
                z_parts[j + one].reshape(2 * G, POINTS) for one in range(width)
            ]
            both = both[0] if width == 1 else jnp.concatenate(both, axis=1)
            values = jnp.dot(y_table[...], both, preferred_element_type=jnp.float32)
            for one in range(width):
                for part in range(2):
                    for high in range(3):
                        lane = one * POINTS + high * 128
                        place = (j + one) * (G * 8) + part * 3 + high
                        coeffs[pl.ds(place, G, stride=8), :] = values[
                            part * G : (part + 1) * G, lane : lane + 128
                        ]

        def two_frequencies(at, carry):
            transform(2 * at, 2)
            return carry

        lax.fori_loop(0, NJ // 2, two_frequencies, 0)
        transform(NJ - 1, 1)

        def fill(target_ref, first, pencils, rows, base):
            def one_target(target, carry):
                pieces = []
                for pencil in range(pencils):
                    slot = slots[0, base + target * pencils + pencil]
                    pieces.append(coeffs[pl.ds(pl.multiple_of(slot * 8, 8), 8), :][:6])
                if rows > 6 * pencils:
                    pieces.append(jnp.zeros((rows - 6 * pencils, 128), jnp.float32))
                target_ref[target] = jnp.concatenate(pieces, axis=0).astype(jnp.bfloat16)
                return carry

            lax.fori_loop(0, DEVICES, one_target, 0, unroll=first)

        fill(out, 8, FIRST, FIRST_ROWS, 0)

        @pl.when(total[0, 0] > DEVICES * FIRST)
        def _():
            fill(more, 1, SECOND, SECOND_ROWS, DEVICES * FIRST)


def plane_chunks(virtual, occupied, occ_index, slots, total):
    smem = pl.BlockSpec(memory_space=pltpu.SMEM)
    whole = lambda *shape: pl.BlockSpec(shape, lambda s: (0,) * len(shape))
    return pl.pallas_call(
        plane_kernel,
        grid=(G // STEP,),
        in_specs=[
            smem,
            smem,
            smem,
            pl.BlockSpec((PLANES, BANDS, STEP * G), lambda s: (0, 0, s)),
            pl.BlockSpec((PLANES, 8, STEP * G), lambda s: (0, 0, s)),
            whole(2, NJ * 8, 4 * G),
            whole(2 * G, 2 * G),
        ],
        out_specs=[whole(DEVICES, FIRST_ROWS, 128), whole(DEVICES, SECOND_ROWS, 128)],
        scratch_shapes=[
            pltpu.VMEM((NJ, 2, G, POINTS), jnp.bfloat16),
            pltpu.VMEM((NJ * G * 8, 128), jnp.float32),
        ],
        out_shape=[
            jax.ShapeDtypeStruct((DEVICES, FIRST_ROWS, 128), jnp.bfloat16),
            jax.ShapeDtypeStruct((DEVICES, SECOND_ROWS, 128), jnp.bfloat16),
        ],
        compiler_params=pltpu.CompilerParams(vmem_limit_bytes=56 * 1024 * 1024),
        name="planes",
    )(
        occ_index,
        slots,
        total,
        virtual,
        occupied,
        jnp.asarray(z_stage_tables(), jnp.bfloat16),
        jnp.asarray(y_stage_table(), jnp.bfloat16),
    )


def swap_halves(first, second, low):
    left = jnp.where(low, first, pltpu.roll(second, 64, 1))
    right = jnp.where(low, pltpu.roll(first, 64, 1), second)
    return left, right


def stack_sources(source, stacked, rows):
    count = FFT * rows
    low = lax.broadcasted_iota(jnp.int32, (count, 128), 1) < 64
    for pair in range(PAIR // 2):
        first = source[:, 2 * pair].astype(jnp.float32).reshape(count, 128)
        second = source[:, 2 * pair + 1].astype(jnp.float32).reshape(count, 128)
        left, right = swap_halves(first, second, low)
        lanes = slice(pair * 128, (pair + 1) * 128)
        stacked[0:count, lanes] = left.astype(jnp.bfloat16)
        stacked[count : 2 * count, lanes] = right.astype(jnp.bfloat16)


def gram_kernel(
    places,
    own,
    total,
    squares,
    weights,
    scale,
    arrived,
    later,
    x_table,
    later_table,
    mine,
    theirs,
    stacked,
    spectra,
    weighted,
    later_here,
    later_stacked,
    sem,
):
    freq = lax.broadcasted_iota(jnp.int32, (2 * G, 128), 0) % G
    freq = (freq + G // 2) % G - G // 2
    squared_x = freq * freq
    exponent = jnp.full((2 * G, 128), scale[0], jnp.float32)
    norm = exponent * G
    norm = norm * jnp.sqrt(norm)

    def transform(table, source, rows, pencils, base, at):
        column = lax.broadcasted_iota(jnp.int32, (2 * G, 2 * FFT * rows), 1) % rows
        for pencil in range(pencils):
            entry = base + pencil
            squared = (squared_x + squares[0, entry]).astype(jnp.float32)
            half = 1.0 / (norm * (1.0 + squared / (exponent * exponent)))
            chosen = jnp.where(column // 6 == pencil, 1.0, 0.0).astype(jnp.bfloat16)
            values = jnp.dot(table[...] * chosen, source[...], preferred_element_type=jnp.float32)
            half = jnp.concatenate([half] * (NBAND // 128), axis=1)
            here = slice((at + pencil) * 2 * G, (at + pencil + 1) * 2 * G)
            rounded = (values * half).astype(jnp.bfloat16)
            spectra[here, :] = rounded
            weighted[here, :] = rounded * jnp.full(
                rounded.shape, weights[0, entry], jnp.float32
            ).astype(jnp.bfloat16)

    stack_sources(arrived, stacked, FIRST_ROWS)
    transform(x_table, stacked, FIRST_ROWS, FIRST, own[0] * FIRST, 0)

    def multiply(pencils):
        low = lax.broadcasted_iota(jnp.int32, (BANDS // 2, 128), 1) < 64
        terms = pencils * 2 * G
        for group in range(4):
            gram = lax.dot_general(
                weighted[:terms, group * 256 : (group + 1) * 256],
                spectra[:terms, :],
                (((0,), (0,)), ((), ())),
                preferred_element_type=jnp.float32,
            )
            for inner in range(4):
                place = places[group * 4 + inner]
                parts = []
                for pair in range(PAIR // 2):
                    tile = gram[inner * 64 : (inner + 1) * 64, pair * 128 : (pair + 1) * 128]
                    parts.extend(swap_halves(tile[:32], tile[32:], low))

                @pl.when(place < PAIR // 2)
                def _():
                    for part in range(PAIR):
                        mine[place, part] = parts[part]

                @pl.when(place >= PAIR // 2)
                def _():
                    for part in range(PAIR):
                        theirs[place - PAIR // 2, part] = parts[part]

    @pl.when(total[0, 0] <= DEVICES * FIRST)
    def _():
        multiply(FIRST)

    @pl.when(total[0, 0] > DEVICES * FIRST)
    def _():
        copy = pltpu.make_async_copy(later, later_here, sem)
        copy.start()
        copy.wait()
        stack_sources(later_here, later_stacked, SECOND_ROWS)
        base = DEVICES * FIRST + own[0] * SECOND
        transform(later_table, later_stacked, SECOND_ROWS, SECOND, base, FIRST)
        multiply(FIRST + SECOND)


def gram_halves(places, own, total, squares, weights, scale, arrived, later):
    half = jax.ShapeDtypeStruct((PAIR // 2, PAIR, 32, 128), jnp.float32)
    smem = pl.BlockSpec(memory_space=pltpu.SMEM)
    vmem = pl.BlockSpec(memory_space=pltpu.VMEM)
    anywhere = pl.BlockSpec(memory_space=pl.ANY)
    terms = (FIRST + SECOND) * 2 * G
    return pl.pallas_call(
        gram_kernel,
        in_specs=[smem] * 6 + [vmem, anywhere, vmem, vmem],
        out_specs=[vmem, vmem],
        out_shape=[half, half],
        scratch_shapes=[
            pltpu.VMEM((2 * FFT * FIRST_ROWS, NBAND), jnp.bfloat16),
            pltpu.VMEM((terms, NBAND), jnp.bfloat16),
            pltpu.VMEM((terms, NBAND), jnp.bfloat16),
            pltpu.VMEM((FFT, PAIR, SECOND_ROWS, 128), jnp.bfloat16),
            pltpu.VMEM((2 * FFT * SECOND_ROWS, NBAND), jnp.bfloat16),
            pltpu.SemaphoreType.DMA,
        ],
        compiler_params=pltpu.CompilerParams(vmem_limit_bytes=56 * 1024 * 1024),
        name="gram",
    )(
        places,
        own,
        total,
        squares,
        weights,
        scale,
        arrived.reshape(FFT, PAIR, FIRST_ROWS, 128),
        later.reshape(FFT, PAIR, SECOND_ROWS, 128),
        jnp.asarray(x_stage_table(FIRST, FIRST_ROWS), jnp.bfloat16),
        jnp.asarray(x_stage_table(SECOND, SECOND_ROWS), jnp.bfloat16),
    )


def body(
    virt_orbitals,
    occ_orbitals,
    occ_index,
    occ_energy,
    band_energy,
    geminal_exponent,
    pencil_index,
    block_owner,
):
    fft_at = lax.axis_index("fft")
    pair_at = lax.axis_index("pair")
    slots, weights, squares, total = pencil_plan(pencil_index)
    chunks, more = plane_chunks(
        jnp.transpose(virt_orbitals, (1, 0, 2)),
        jnp.transpose(occ_orbitals, (1, 0, 2)),
        occ_index,
        slots,
        total,
    )

    def exchanged(sent):
        return lax.all_to_all(sent, ("fft", "pair"), split_axis=0, concat_axis=0, tiled=True)

    arrived = exchanged(chunks)
    later = lax.cond(total[0, 0] > DEVICES * FIRST, exchanged, jnp.zeros_like, more)

    order = jnp.arange(PAIR, dtype=jnp.int32)
    owner = jnp.sum(
        jnp.where(block_owner[:, None] == order[None, :], order[:, None], 0), axis=0
    )
    places = owner // 2 + jnp.where(owner % 2 == pair_at % 2, 0, PAIR // 2)
    own = jnp.reshape(fft_at * PAIR + pair_at, (1,))
    mine, theirs = gram_halves(
        places, own, total, squares, weights, geminal_exponent, arrived, later
    )
    swapped = lax.ppermute(theirs, "pair", [(i, i ^ 1) for i in range(PAIR)])
    same_core = [list(range(0, PAIR, 2)), list(range(1, PAIR, 2))]
    rows = lax.all_to_all(
        mine + swapped, "pair", 0, 0, tiled=True, axis_index_groups=same_core
    ).sum(axis=0)
    total = lax.all_to_all(rows, "fft", 0, 0, tiled=True).sum(axis=0)
    gram = jnp.concatenate([total[:, :64], total[:, 64:]], axis=0)
    block = lax.dynamic_index_in_dim(block_owner, pair_at, keepdims=False)
    row_energy = lax.dynamic_slice_in_dim(band_energy, block * BANDS, BANDS)
    column_energy = lax.dynamic_slice_in_dim(band_energy, fft_at * BANDS, BANDS)
    occupied_energy = lax.dynamic_index_in_dim(occ_energy, occ_index[0], keepdims=False)
    return (row_energy[:, None] + column_energy[None, :] - 2.0 * occupied_energy) * gram


def solution(mesh):
    return jax.shard_map(
        body,
        mesh=mesh,
        in_specs=(P("pair", "fft", None), P(None, "fft", None), P(), P(), P(), P(), P(), P()),
        out_specs=P("pair", "fft"),
        check_vma=False,
    )
```

time: 168 us -> 141 us (0.84)
  waiting for transfers between devices: 70.3 us -> 50.6 us
  Pallas kernels: 30.4 us -> 25 us
  other arithmetic: 8.29 us -> 4.31 us
    all_to_all x1, waiting for transfers between devices: 59.7 us -> 40 us  [exchanged(): lax.all_to_all(sent, ('fft', 'pair'), split_axis=0, concat_axis=0, tiled=...]
    pallas_call x2 -> x3, Pallas kernels: 30.4 us -> 25 us  [the longest x1 12.5 us: plane_chunks(): pl.pallas_call(plane_kernel, grid=(G // STEP,), in_specs=[smem, smem, sme...]
    add x2 -> x0, other arithmetic: 2.69 us -> none  [the longest x1 1.37 us: body(): freq_y * freq_y + freq_z * freq_z]
  transfers between devices with their start and end apart: 3 -> 3, of which waited for: 3 -> 3; matrix products, arithmetic and copies ran while one was open for 3% -> 2% of each run, Pallas kernels for 0% -> 0%
where the time goes in v2:
time: 141 us
  waiting for transfers between devices  50.6 us (36%)
  blocking collectives  31.7 us (22%)
  Pallas kernels  25 us (18%)
  starting transfers between devices  20.9 us (15%)
  local copies, waits for them, and re-layouts  4.77 us (3%)
  other arithmetic  4.31 us (3%)
  between operations  3.28 us (2%)
    all_to_all x1, waiting for transfers between devices, exchanged(): lax.all_to_all(sent, ('fft', 'pair'), split_axis=0, concat_axis=0, tiled=...  40 us
    all_to_all x1, blocking collectives, body(): lax.all_to_all(mine + swapped, 'pair', 0, 0, tiled=True, axis_index_group...  31.7 us
    all_to_all x1, starting transfers between devices, exchanged(): lax.all_to_all(sent, ('fft', 'pair'), split_axis=0, concat_axis=0, tiled=...  14.7 us
    pallas_call x1, Pallas kernels, plane_chunks(): pl.pallas_call(plane_kernel, grid=(G // STEP,), in_specs=[smem, smem, sme...  12.5 us
    pallas_call x1, Pallas kernels, gram_halves(): pl.pallas_call(gram_kernel, in_specs=[smem] * 6 + [vmem, anywhere, vmem,...  10.1 us
    all_to_all x1, waiting for transfers between devices, body(): total = lax.all_to_all(rows, 'fft', 0, 0, tiled=True).sum(axis=0)  6.6 us
    all_to_all x1, starting transfers between devices, body(): total = lax.all_to_all(rows, 'fft', 0, 0, tiled=True).sum(axis=0)  4.8 us
    ppermute x1, waiting for transfers between devices, body(): swapped = lax.ppermute(theirs, 'pair', [(i, i ^ 1) for i in range(PAIR)])  4 us
  transfers between devices with their start and end apart: 3, of which 3 were waited for; matrix products, arithmetic and copies ran while one was open for 2% of the time, Pallas kernels for 0%

profile of v2, /device:TPU:2, one launch (start us, length us, event | category | flops | bytes accessed | tf_op | source)
XLA Modules:
  0.0 140.6 jit_solution(3286754714145760326)
XLA Ops:
  0.7 1.3 reshape.26.pencils
  1.9 2.4 %plan.1 = (s32[1,1536]{1,0:T(1,128)}, f32[1,1536]{1,0:T(1,128)}, s32[1,1536]{1,0:T(1,128)}, s32[1,128]{1,0:T(1,128)}) custom-call(s32[1,1536]{1,0:T(1,128)} %reshape.26.pencils), custom_call_target="tpu_custom_call" | custom-call | tf_op jit(solution)/shard_map/plan/pallas_call | solution.py:123
  4.9 12.5 %planes.1 = (bf16[256,24,128]{2,1,0:T(8,128)(2,1)}, bf16[256,16,128]{2,1,0:T(8,128)(2,1)S(1)}) custom-call(s32[1]{0:T(128)} %copy.15.occ_index, s32[1,1536]{1,0:T(1,128)} %get-tuple-element.21.slots, s32[1,128]{1,0:T(1,128)} %get-tuple-element.18.total, bf16[6,64,9216]{2,1,0:T(8,128)(2,1)} %bitcast.13, bf16[6,8,9216]{2,1,0:T(8,128)(2,1)} %bitcast.16, ...), custom_call_target="tpu_custom_call" | custom-call | tf_op jit(solution)/shard_map/planes/pallas_call | solution.py:219
  17.4 0.2 conditional.1
  17.4 0.2 reshape.20
  17.6 0.0 copy-start.1
  17.6 14.7 %all-to-all-start.1 = ((bf16[256,24,128]{2,1,0:T(8,128)(2,1)}), bf16[256,24,128]{2,1,0:T(8,128)(2,1)S(1)}, u32[]{:S(2)}, u32[]{:S(2)}) async-start(bf16[256,24,128]{2,1,0:T(8,128)(2,1)} %get-tuple-element.22), calls=%async_computation.1 | async-start | bytes 3145728 | tf_op jit(solution)/shard_map/all_to_all | solution.py:416
  33.0 0.0 copy-done.1
  33.0 0.1 select_reduce_fusion
  33.1 0.5 fusion.places
  33.6 40.0 %all-to-all-done.1 = bf16[256,24,128]{2,1,0:T(8,128)(2,1)S(1)} async-done(((bf16[256,24,128]{2,1,0:T(8,128)(2,1)}), bf16[256,24,128]{2,1,0:T(8,128)(2,1)S(1)}, u32[]{:S(2)}, u32[]{:S(2)}) %all-to-all-start.1) | async-done | bytes 1572896 | tf_op jit(solution)/shard_map/all_to_all | solution.py:416
  73.6 0.0 copy-start
  73.6 1.2 copy-done
  74.8 10.1 %gram.1 = (f32[8,16,32,128]{3,2,1,0:T(8,128)}, f32[8,16,32,128]{3,2,1,0:T(8,128)}) custom-call(s32[16]{0:T(128)} %fusion.places, s32[1]{0:T(128)} %bitcast.4.own, s32[1,128]{1,0:T(1,128)} %get-tuple-element.18.total, s32[1,1536]{1,0:T(1,128)} %get-tuple-element.19.squares, f32[1,1536]{1,0:T(1,128)} %get-tuple-element.20.weights, f32[1]{0:T(128)S(6)} %copy.16.scale, ...), custom_call_target="tpu_custom_call" | custom-call | tf_op jit(solution)/shard_map/gram/pallas_call | solution.py:365
  85.0 1.5 %collective-permute-start = (f32[8,16,32,128]{3,2,1,0:T(8,128)}, f32[8,16,32,128]{3,2,1,0:T(8,128)S(1)}, u32[]{:S(2)}, u32[]{:S(2)}) collective-permute-start(f32[8,16,32,128]{3,2,1,0:T(8,128)} %get-tuple-element.25), channel_id=1, source_target_pairs={{0,1},{1,0},{2,3},{3,2},{4,5},{5,4},{6,7},{7,6},{8,9},{9,8},{10,11... | collective-permute-start | bytes 6291464 | tf_op jit(solution)/shard_map/ppermute | solution.py:430
  86.4 4.0 %collective-permute-done = f32[8,16,32,128]{3,2,1,0:T(8,128)S(1)} collective-permute-done((f32[8,16,32,128]{3,2,1,0:T(8,128)}, f32[8,16,32,128]{3,2,1,0:T(8,128)S(1)}, u32[]{:S(2)}, u32[]{:S(2)}) %collective-permute-start) | collective-permute-done | bytes 2097184 | tf_op jit(solution)/shard_map/ppermute | solution.py:430
  90.4 2.1 %add.58 = f32[8,16,32,128]{3,2,1,0:T(8,128)S(1)} add(f32[8,16,32,128]{3,2,1,0:T(8,128)} %get-tuple-element.24, f32[8,16,32,128]{3,2,1,0:T(8,128)S(1)} %collective-permute-done) | non-fusion elementwise | flops 524288 | bytes 6291456 | tf_op jit(solution)/shard_map/add | solution.py:433
  92.5 31.7 %all_to_all.20 = f32[8,16,32,128]{3,2,1,0:T(8,128)S(1)} all-to-all(f32[8,16,32,128]{3,2,1,0:T(8,128)S(1)} %add.58), channel_id=1, replica_groups={{0,2,4,6,8,10,12,14},{1,3,5,7,9,11,13,15},{16,18,20,22,24,26,28,30},{17..., dimensions={0} | all-to-all | bytes 4194304 | tf_op jit(solution)/shard_map/all_to_all | solution.py:432
  124.2 0.0 copy-start.2
  124.2 0.9 reduce_sum.28
  125.1 4.8 %all-to-all-start.3 = ((f32[16,32,128]{2,1,0:T(8,128)}), f32[16,32,128]{2,1,0:T(8,128)S(1)}, u32[]{:S(2)}, u32[]{:S(2)}) async-start(f32[16,32,128]{2,1,0:T(8,128)} %reduce_sum.28), calls=%async_computation.3 | async-start | bytes 524288 | tf_op jit(solution)/shard_map/all_to_all | solution.py:435
  129.9 0.6 dynamic_slice.14
  131.1 0.0 copy-done.2
  131.2 0.6 dynamic_slice.17
  132.4 0.8 fusion.2
  133.2 6.6 %all-to-all-done.3 = f32[16,32,128]{2,1,0:T(8,128)S(1)} async-done(((f32[16,32,128]{2,1,0:T(8,128)}), f32[16,32,128]{2,1,0:T(8,128)S(1)}, u32[]{:S(2)}, u32[]{:S(2)}) %all-to-all-start.3) | async-done | bytes 262176 | tf_op jit(solution)/shard_map/all_to_all | solution.py:435
  139.9 0.1 fusion.1
  139.9 0.7 maximum_multiply_fusion
  (1 shorter events, 0.0 us)
Async XLA Ops:
  17.6 15.4 %copy-start.1 = (s32[16]{0:T(128)S(1)}, s32[16]{0:T(128)}, u32[]{:S(2)}) copy-start(s32[16]{0:T(128)} %param.21) | copy-start | bytes 196
  17.6 56.0 %all-to-all-start.1 = ((bf16[256,24,128]{2,1,0:T(8,128)(2,1)}), bf16[256,24,128]{2,1,0:T(8,128)(2,1)S(1)}, u32[]{:S(2)}, u32[]{:S(2)}) async-start(bf16[256,24,128]{2,1,0:T(8,128)(2,1)} %get-tuple-element.22), calls=%async_computation.1 | async-start | bytes 3145728 | tf_op jit(solution)/shard_map/all_to_all | solution.py:416
  73.6 1.2 copy-start
  85.0 5.5 %collective-permute-start = (f32[8,16,32,128]{3,2,1,0:T(8,128)}, f32[8,16,32,128]{3,2,1,0:T(8,128)S(1)}, u32[]{:S(2)}, u32[]{:S(2)}) collective-permute-start(f32[8,16,32,128]{3,2,1,0:T(8,128)} %get-tuple-element.25), channel_id=1, source_target_pairs={{0,1},{1,0},{2,3},{3,2},{4,5},{5,4},{6,7},{7,6},{8,9},{9,8},{10,11... | collective-permute-start | bytes 6291464 | tf_op jit(solution)/shard_map/ppermute | solution.py:430
  124.2 7.0 %copy-start.2 = (f32[8]{0:T(128)S(1)}, f32[8]{0:T(128)}, u32[]{:S(2)}) copy-start(f32[8]{0:T(128)} %param.17) | copy-start | bytes 100
  125.1 14.7 %all-to-all-start.3 = ((f32[16,32,128]{2,1,0:T(8,128)}), f32[16,32,128]{2,1,0:T(8,128)S(1)}, u32[]{:S(2)}, u32[]{:S(2)}) async-start(f32[16,32,128]{2,1,0:T(8,128)} %reduce_sum.28), calls=%async_computation.3 | async-start | bytes 524288 | tf_op jit(solution)/shard_map/all_to_all | solution.py:435
